TPU v7x, 32 devices: a whole 2x2x4 slice. The times are simulated.
32 devices in a mesh: ctx: 4 (over y, x), fsdp: 8 (over z, core).
Axes of the slice: x: 2, y: 2, z: 4, core: 2. Of those that a mesh axis runs over, the one named last changes fastest.
Arguments:
- layer_input: bfloat16 [1280, 4, 1536], P(('ctx', 'fsdp')), may hold values from -6 to 6
- block_order: int32 [2, 8], replicated, may hold values from 0 to 7, each once within a row
- first_gain: bfloat16 [1536], P('fsdp'), may hold values from 0.25 to 1.75
- w_qkv: bfloat16 [1536, 2048], P('fsdp'), may hold values from -0.15625 to 0.15625
- b_qkv: bfloat16 [2048], P('fsdp'), may hold values from -1.5 to 1.5
- w_o: bfloat16 [1536, 1536], P('fsdp'), may hold values from -1.25 to 1.25
- second_gain: bfloat16 [1536], P('fsdp'), may hold values from 0.25 to 1.75
- w_gate: bfloat16 [1536, 8960], P('fsdp'), may hold values from -0.15625 to 0.15625
- w_up: bfloat16 [1536, 8960], P('fsdp'), may hold values from -0.15625 to 0.15625
- w_down: bfloat16 [8960, 1536], P('fsdp'), may hold values from -0.0625 to 0.0625
- cotangent: bfloat16 [1280, 4, 1536], P(('ctx', 'fsdp')), may hold values from -6 to 6
Outputs:
- mixed: bfloat16 [1280, 4, 1536], P(('ctx', 'fsdp'))
- input_grad: float32 [1280, 4, 1536], P(('ctx', 'fsdp'))
- first_gain_grad: float32 [1536], P('fsdp')
- w_qkv_grad: float32 [1536, 2048], P('fsdp')
- b_qkv_grad: float32 [1792], P('fsdp')
- value_bias_grad: float32 [256], P('fsdp')
- w_o_grad: float32 [1536, 1536], P('fsdp')
- second_gain_grad: float32 [1536], P('fsdp')
- w_gate_grad: float32 [1536, 8960], P('fsdp')
- w_up_grad: float32 [1536, 8960], P('fsdp')
- w_down_grad: float32 [8960, 1536], P('fsdp')
Inputs may be any that keep to these rules, and one draw needn't show every extreme that they name: `block_order`: each row is a permutation.
All inputs are finite; a program needn't handle non-finite values.
Results may differ from a plain program's by a relative error of at most 0.02.
Values may be sent and summed in bfloat16 or wider, within the bound.
A program may use at most 576 MiB of HBM per device.

v0:
```python
import math
import jax
import jax.numpy as jnp
from jax import lax
from jax.sharding import PartitionSpec as P

D = 1536
H = 12
KVH = 2
HD = 128
FF = 8960
SEQS = 2
QKV = 2048
QK = 1792
EPS = 1e-06
THETA = 1000000.0
KEY_BLOCK = 256
NEG_FILL = -1e30
CONTRACT_LAST = (((1,), (1,)), ((), ()))
CONTRACT_FIRST = (((0,), (0,)), ((), ()))


def narrowed(values):
    return lax.optimization_barrier(values.astype(jnp.bfloat16)).astype(jnp.float32)


def block_positions(block_order, first_row, row_count, block_rows, ctx_size):
    row_index = first_row + jnp.arange(row_count, dtype=jnp.int32)
    slot_index = jnp.arange(2 * SEQS, dtype=jnp.int32)
    entries = (slot_index // SEQS)[None, :] * ctx_size + (row_index // block_rows)[:, None]
    tiled = jnp.tile(block_order, (2, 1))
    entry_ids = jnp.arange(2 * ctx_size, dtype=jnp.int32)
    picked = jnp.sum(
        jnp.where(entries[:, :, None] == entry_ids[None, None, :], tiled[None, :, :], 0), -1
    )
    return picked * block_rows + (row_index % block_rows)[:, None]


def pos_groups(positions):
    row_count = positions.shape[0]
    return positions.reshape(row_count, 2, SEQS).transpose(2, 0, 1).reshape(SEQS, row_count * 2)


def to_groups(tokens, row_count, group_size):
    shaped = tokens.reshape(row_count, 2, SEQS, KVH, group_size, HD)
    return shaped.transpose(2, 3, 4, 0, 1, 5).reshape(SEQS, KVH, group_size * row_count * 2, HD)


def from_groups(grouped, row_count, group_size):
    shaped = grouped.reshape(SEQS, KVH, group_size, row_count, 2, HD).transpose(3, 4, 0, 1, 2, 5)
    return shaped.reshape(row_count * 2 * SEQS, KVH * group_size * HD)


def rope_tables(positions):
    half_width = HD // 2
    frequency = THETA ** (-jnp.arange(half_width, dtype=jnp.float32) * 2.0 / HD)
    angles = positions.astype(jnp.float32)[:, None] * frequency[None, :]
    cosine_table = jnp.concatenate([jnp.cos(angles), jnp.cos(angles)], -1)[:, None, :]
    sine_table = jnp.concatenate([jnp.sin(angles), jnp.sin(angles)], -1)[:, None, :]
    return (cosine_table, sine_table)


def rotate(head_values, cosine_table, sine_table):
    half_width = HD // 2
    turned = jnp.concatenate([-head_values[..., half_width:], head_values[..., :half_width]], -1)
    return head_values * cosine_table + turned * sine_table


def rotate_back(grad_values, cosine_table, sine_table):
    half_width = HD // 2
    moved = grad_values * sine_table
    return grad_values * cosine_table + jnp.concatenate(
        [moved[..., half_width:], -moved[..., :half_width]], -1
    )


def normalize(values, gain):
    scale = lax.rsqrt(jnp.mean(values * values, -1, keepdims=True) + EPS)
    unit = values * scale
    return (unit, scale, unit * gain)


def norm_back(grad_out, unit, scale, gain):
    grad_unit = grad_out * gain
    inner = jnp.mean(grad_unit * unit, -1, keepdims=True)
    return (scale * (grad_unit - unit * inner), jnp.sum(grad_out * unit, 0))


def split_blocks(piece):
    row_count = piece.shape[0]
    size = math.gcd(row_count, KEY_BLOCK)
    stacked = piece.reshape(row_count // size, size, piece.shape[1], piece.shape[2])
    firsts = size * jnp.arange(row_count // size, dtype=jnp.int32)
    return (stacked, firsts)


def shards(
    layer_input,
    block_order,
    first_gain,
    w_qkv,
    b_qkv,
    w_o,
    second_gain,
    w_gate,
    w_up,
    w_down,
    cotangent,
):
    ctx_size = lax.axis_size("ctx")
    shard_count = lax.axis_size("fsdp")
    rows_here = layer_input.shape[0]
    slots = layer_input.shape[1]
    block_rows = rows_here * shard_count
    group_size = H // KVH
    kv_width = KVH * HD
    first_row = (lax.axis_index("ctx") * shard_count + lax.axis_index("fsdp")) * rows_here
    own_pos = block_positions(block_order, first_row, rows_here, block_rows, ctx_size)
    cosine_table, sine_table = rope_tables(own_pos.reshape(-1))
    query_scale = HD ** (-0.5)
    w_qkv_all, w_o_all, bias_all, gain_one, gain_two = (
        lax.all_gather(w_qkv, "fsdp", axis=0, tiled=True),
        lax.all_gather(w_o, "fsdp", axis=0, tiled=True),
        lax.all_gather(b_qkv, "fsdp", axis=0, tiled=True),
        lax.all_gather(first_gain, "fsdp", axis=0, tiled=True),
        lax.all_gather(second_gain, "fsdp", axis=0, tiled=True),
    )
    gain_one = gain_one.astype(jnp.float32)
    gain_two = gain_two.astype(jnp.float32)
    inputs = layer_input.reshape(-1, D).astype(jnp.float32)
    unit_one, scale_one, normed = normalize(inputs, gain_one)
    normed_one = normed.astype(jnp.bfloat16)
    projected = jnp.dot(
        normed_one, w_qkv_all, preferred_element_type=jnp.float32
    ) + bias_all.astype(jnp.float32)
    query_raw = projected[:, : H * HD].reshape(-1, H, HD)
    key_raw = projected[:, H * HD : H * HD + kv_width].reshape(-1, KVH, HD)
    value_raw = projected[:, H * HD + kv_width :]
    query_tokens = (
        (rotate(query_raw, cosine_table, sine_table) * query_scale)
        .astype(jnp.bfloat16)
        .reshape(-1, H * HD)
    )
    key_tokens = (
        rotate(key_raw, cosine_table, sine_table).astype(jnp.bfloat16).reshape(-1, kv_width)
    )
    own_kv = jnp.concatenate([key_tokens, value_raw.astype(jnp.bfloat16)], -1).reshape(
        rows_here, slots, 2 * kv_width
    )
    block_kv = lax.all_gather(own_kv, "fsdp", axis=0, tiled=True)
    queries = to_groups(query_tokens, rows_here, group_size)
    query_pos = jnp.tile(pos_groups(own_pos), (1, group_size))
    query_count = queries.shape[2]

    def piece_keys(key_rows, row_start):
        row_count = key_rows.shape[0]
        flat = key_rows.reshape(row_count * slots, 2 * kv_width)
        keys_grouped = to_groups(flat[:, :kv_width], row_count, 1)
        values_grouped = to_groups(flat[:, kv_width:], row_count, 1)
        key_pos = pos_groups(
            block_positions(block_order, row_start, row_count, block_rows, ctx_size)
        )
        visible = query_pos[:, None, :, None] >= key_pos[:, None, None, :]
        scores = jnp.einsum(
            "snmd,snkd->snmk", queries, keys_grouped, preferred_element_type=jnp.float32
        )
        return (keys_grouped, values_grouped, visible, scores)

    start_state = (
        jnp.full((SEQS, KVH, query_count), NEG_FILL, jnp.float32),
        jnp.zeros((SEQS, KVH, query_count), jnp.float32),
        jnp.zeros((SEQS, KVH, query_count, HD), jnp.float32),
    )
    state = start_state
    stacked, firsts = split_blocks(lax.all_gather(block_kv, "ctx", axis=0, tiled=True))

    def forward_one_block(carry, item):
        best, totals, accum = carry
        key_rows, row_start = item
        keys_grouped, values_grouped, visible, scores = piece_keys(key_rows, row_start)
        scores = jnp.where(visible, scores, NEG_FILL)
        fresh = jnp.maximum(best, jnp.max(scores, -1))
        weights = jnp.where(visible, jnp.exp(scores - fresh[..., None]), 0.0)
        decay = jnp.exp(best - fresh)
        totals = totals * decay + jnp.sum(weights, -1)
        accum = accum * decay[..., None] + jnp.einsum(
            "snmk,snkd->snmd",
            weights.astype(jnp.bfloat16),
            values_grouped,
            preferred_element_type=jnp.float32,
        )
        return ((fresh, totals, accum), None)

    state, unused = lax.scan(forward_one_block, state, (stacked, firsts))
    best, totals, accum = state
    attended_grouped = accum / totals[..., None]
    logsum = best + jnp.log(totals)
    attended_low = from_groups(attended_grouped, rows_here, group_size).astype(jnp.bfloat16)
    middle = inputs + jnp.dot(attended_low, w_o_all, preferred_element_type=jnp.float32)
    unit_two, scale_two, normed = normalize(middle, gain_two)
    normed_two = normed.astype(jnp.bfloat16)
    gate_all, up_all, down_all = (
        lax.all_gather(w_gate, "fsdp", axis=0, tiled=True),
        lax.all_gather(w_up, "fsdp", axis=0, tiled=True),
        lax.all_gather(w_down, "fsdp", axis=0, tiled=True),
    )
    gate_part = jnp.dot(normed_two, gate_all, preferred_element_type=jnp.float32)
    up_part = jnp.dot(normed_two, up_all, preferred_element_type=jnp.float32)
    activated = jax.nn.silu(gate_part)
    hidden = (activated * up_part).astype(jnp.bfloat16)
    mixed_out = middle + jnp.dot(hidden, down_all, preferred_element_type=jnp.float32)
    output = mixed_out.astype(jnp.bfloat16).reshape(rows_here, slots, D)
    gate_all, up_all, down_all = (
        lax.all_gather(w_gate, "fsdp", axis=0, tiled=True),
        lax.all_gather(w_up, "fsdp", axis=0, tiled=True),
        lax.all_gather(w_down, "fsdp", axis=0, tiled=True),
    )
    w_qkv_all, w_o_all = (
        lax.all_gather(w_qkv, "fsdp", axis=0, tiled=True),
        lax.all_gather(w_o, "fsdp", axis=0, tiled=True),
    )
    grad_branch_two = cotangent.reshape(-1, D)
    grad_hidden = lax.dot_general(
        grad_branch_two, down_all, CONTRACT_LAST, preferred_element_type=jnp.float32
    )
    sigmoid_gate = jax.nn.sigmoid(gate_part)
    grad_gate = grad_hidden * up_part * sigmoid_gate * (1.0 + gate_part * (1.0 - sigmoid_gate))
    grad_gate_up = jnp.concatenate([grad_gate, grad_hidden * activated], -1).astype(jnp.bfloat16)
    grad_normed_two = lax.dot_general(
        grad_gate_up[:, :FF], gate_all, CONTRACT_LAST, preferred_element_type=jnp.float32
    )
    grad_normed_two = grad_normed_two + lax.dot_general(
        grad_gate_up[:, FF:], up_all, CONTRACT_LAST, preferred_element_type=jnp.float32
    )
    grad_middle_norm, grad_gain_two = norm_back(grad_normed_two, unit_two, scale_two, gain_two)
    grad_middle = cotangent.reshape(-1, D).astype(jnp.float32) + grad_middle_norm
    grad_branch_one = grad_middle.astype(jnp.bfloat16)
    grad_attended = lax.dot_general(
        grad_branch_one, w_o_all, CONTRACT_LAST, preferred_element_type=jnp.float32
    ).astype(jnp.bfloat16)
    grad_out_grouped = to_groups(grad_attended, rows_here, group_size)
    delta = jnp.sum(grad_out_grouped.astype(jnp.float32) * attended_grouped, -1)
    back_state = (
        jnp.zeros((SEQS, KVH, query_count, HD), jnp.float32),
        jnp.zeros((ctx_size * block_rows, slots, 2 * kv_width), jnp.float32),
    )
    state = back_state
    stacked, firsts = split_blocks(lax.all_gather(block_kv, "ctx", axis=0, tiled=True))

    def backward_one_block(carry, item):
        grad_queries, grad_kv_full = carry
        key_rows, row_start = item
        row_count = key_rows.shape[0]
        keys_grouped, values_grouped, visible, scores = piece_keys(key_rows, row_start)
        probs = jnp.where(
            visible, jnp.exp(jnp.where(visible, scores, NEG_FILL) - logsum[..., None]), 0.0
        )
        grad_probs = jnp.einsum(
            "snmd,snkd->snmk", grad_out_grouped, values_grouped, preferred_element_type=jnp.float32
        )
        grad_scores = (probs * (grad_probs - delta[..., None])).astype(jnp.bfloat16)
        grad_queries = grad_queries + jnp.einsum(
            "snmk,snkd->snmd", grad_scores, keys_grouped, preferred_element_type=jnp.float32
        )
        grad_keys = jnp.einsum(
            "snmk,snmd->snkd", grad_scores, queries, preferred_element_type=jnp.float32
        )
        grad_values = jnp.einsum(
            "snmk,snmd->snkd",
            probs.astype(jnp.bfloat16),
            grad_out_grouped,
            preferred_element_type=jnp.float32,
        )
        block_terms = jnp.concatenate(
            [from_groups(grad_keys, row_count, 1), from_groups(grad_values, row_count, 1)], -1
        ).reshape(row_count, slots, 2 * kv_width)
        previous = lax.dynamic_slice_in_dim(grad_kv_full, row_start, row_count, 0)
        grad_kv_full = lax.dynamic_update_slice_in_dim(
            grad_kv_full, previous + block_terms, row_start, 0
        )
        return ((grad_queries, grad_kv_full), None)

    state, unused = lax.scan(backward_one_block, state, (stacked, firsts))
    grad_queries, grad_kv_full = state
    grad_kv = lax.psum_scatter(grad_kv_full, ("ctx", "fsdp"), scatter_dimension=0, tiled=True)
    grad_kv_low = narrowed(grad_kv).reshape(-1, 2 * kv_width)
    grad_query_tokens = from_groups(narrowed(grad_queries), rows_here, group_size) * query_scale
    grad_query_raw = rotate_back(
        grad_query_tokens.reshape(-1, H, HD), cosine_table, sine_table
    ).reshape(-1, H * HD)
    grad_key_raw = rotate_back(
        grad_kv_low[:, :kv_width].reshape(-1, KVH, HD), cosine_table, sine_table
    ).reshape(-1, kv_width)
    grad_projected = jnp.concatenate(
        [grad_query_raw, grad_key_raw, grad_kv_low[:, kv_width:]], -1
    ).astype(jnp.bfloat16)
    grad_bias = jnp.sum(grad_projected, 0, dtype=jnp.float32)
    grad_bias_qk = grad_bias[:QK]
    grad_bias_value = grad_bias[QK:]
    grad_normed_one = lax.dot_general(
        grad_projected, w_qkv_all, CONTRACT_LAST, preferred_element_type=jnp.float32
    )
    grad_input_norm, grad_gain_one = norm_back(grad_normed_one, unit_one, scale_one, gain_one)
    grad_input = (grad_middle + grad_input_norm).reshape(rows_here, slots, D)
    weight_rows = lax.psum_scatter(
        jnp.concatenate(
            [
                lax.dot_general(
                    normed_two, grad_gate_up, CONTRACT_FIRST, preferred_element_type=jnp.float32
                ),
                lax.dot_general(
                    normed_one, grad_projected, CONTRACT_FIRST, preferred_element_type=jnp.float32
                ),
                lax.dot_general(
                    attended_low,
                    grad_branch_one,
                    CONTRACT_FIRST,
                    preferred_element_type=jnp.float32,
                ),
            ],
            1,
        ).astype(jnp.bfloat16),
        "fsdp",
        scatter_dimension=0,
        tiled=True,
    ).astype(jnp.float32)
    down_rows = lax.psum_scatter(
        lax.dot_general(
            hidden, grad_branch_two, CONTRACT_FIRST, preferred_element_type=jnp.float32
        ).astype(jnp.bfloat16),
        "fsdp",
        scatter_dimension=0,
        tiled=True,
    ).astype(jnp.float32)
    gain_one_rows, gain_two_rows, bias_rows, value_bias_rows = (
        lax.psum_scatter(grad_gain_one, "fsdp", scatter_dimension=0, tiled=True),
        lax.psum_scatter(grad_gain_two, "fsdp", scatter_dimension=0, tiled=True),
        lax.psum_scatter(grad_bias_qk, "fsdp", scatter_dimension=0, tiled=True),
        lax.psum_scatter(grad_bias_value, "fsdp", scatter_dimension=0, tiled=True),
    )
    weight_rows, down_rows, gain_one_rows, gain_two_rows, bias_rows, value_bias_rows = (
        lax.psum(weight_rows.astype(jnp.bfloat16), "ctx").astype(jnp.float32),
        lax.psum(down_rows.astype(jnp.bfloat16), "ctx").astype(jnp.float32),
        lax.psum(gain_one_rows.astype(jnp.bfloat16), "ctx").astype(jnp.float32),
        lax.psum(gain_two_rows.astype(jnp.bfloat16), "ctx").astype(jnp.float32),
        lax.psum(bias_rows.astype(jnp.bfloat16), "ctx").astype(jnp.float32),
        lax.psum(value_bias_rows.astype(jnp.bfloat16), "ctx").astype(jnp.float32),
    )
    return (
        output,
        grad_input,
        gain_one_rows,
        weight_rows[:, 2 * FF : 2 * FF + QKV],
        bias_rows,
        value_bias_rows,
        weight_rows[:, 2 * FF + QKV :],
        gain_two_rows,
        weight_rows[:, :FF],
        weight_rows[:, FF : 2 * FF],
        down_rows,
    )


def solution(mesh):
    in_specs = (
        P(("ctx", "fsdp"), None, None),
        P(),
        P("fsdp"),
        P("fsdp", None),
        P("fsdp"),
        P("fsdp", None),
        P("fsdp"),
        P("fsdp", None),
        P("fsdp", None),
        P("fsdp", None),
        P(("ctx", "fsdp"), None, None),
    )
    out_specs = (
        P(("ctx", "fsdp"), None, None),
        P(("ctx", "fsdp"), None, None),
        P("fsdp"),
        P("fsdp", None),
        P("fsdp"),
        P("fsdp"),
        P("fsdp", None),
        P("fsdp"),
        P("fsdp", None),
        P("fsdp", None),
        P("fsdp", None),
    )
    return jax.shard_map(shards, mesh=mesh, in_specs=in_specs, out_specs=out_specs, check_vma=False)
```

profile of v0, /device:TPU:0, one launch (start us, length us, event | category | flops | bytes accessed | tf_op | source)
XLA Modules:
  0.0 2331.6 jit_solution(8139246037101609936)
XLA Ops:
  9.8 13.5 all-gather
  27.0 15.6 all-reduce.8
  46.4 31.2 %all-gather.9.cloned.1.call-done = bf16[1536,2048]{1,0:T(8,128)(2,1)} async-done(((bf16[192,2048]{1,0:T(8,128)(2,1)}), bf16[1536,2048]{1,0:T(8,128)(2,1)}) %all-gather.9.cloned.1.call-update) | async-done | bytes 6291472 | tf_op jit(solution)/shard_map/all_gather | solution.py:122
  84.0 22.2 all-gather.11.cloned.1.call-done
  125.7 43.1 %all-gather.13.cloned.1.call-done = bf16[1280,4,512]{2,1,0:T(4,128)(2,1)} async-done(((bf16[320,4,512]{2,1,0:T(4,128)(2,1)}), bf16[1280,4,512]{2,1,0:T(4,128)(2,1)}) %all-gather.13.cloned.1.call-update) | async-done | bytes 5242896 | tf_op jit(solution)/shard_map/all_gather | solution.py:175
  168.8 82.5 %while.34 = (s32[]{:T(128)}, f32[2,2,480]{2,1,0:T(2,128)S(1)}, f32[2,2,480]{2,1,0:T(2,128)S(1)}, f32[2,2,480,128]{3,2,1,0:T(8,128)}, s32[5]{0:T(128)S(1)}, /*ind...) while((s32[]{:T(128)}, f32[2,2,480]{2,1,0:T(2,128)S(1)}, ...), condition=%wide.region_6.7_spmd.clone, body=%wide.region_2.6_spmd.clone.sunk | while | flops 514415264 | bytes 27955316 | solution.py:194
  257.4 203.6 %all-gather.17.cloned.1.call-done = bf16[1536,8960]{1,0:T(8,128)(2,1)} async-done(((bf16[192,8960]{1,0:T(8,128)(2,1)}), bf16[1536,8960]{1,0:T(8,128)(2,1)}) %all-gather.17.cloned.1.call-update) | async-done | bytes 27525136 | tf_op jit(solution)/shard_map/all_gather | solution.py:203
  461.0 16.3 fusion.69
  477.3 222.6 %all-gather.19.cloned.1.call-done = bf16[1536,8960]{1,0:T(8,128)(2,1)} async-done(((bf16[192,8960]{1,0:T(8,128)(2,1)}), bf16[1536,8960]{1,0:T(8,128)(2,1)}) %all-gather.19.cloned.1.call-update) | async-done | bytes 27525136 | tf_op jit(solution)/shard_map/all_gather | solution.py:204
  699.9 16.4 fusion.70
  716.4 222.6 %all-gather.21.cloned.1.call-done = bf16[8960,1536]{1,0:T(8,128)(2,1)} async-done(((bf16[1120,1536]{1,0:T(8,128)(2,1)}), bf16[8960,1536]{1,0:T(8,128)(2,1)}) %all-gather.21.cloned.1.call-update) | async-done | bytes 27525136 | tf_op jit(solution)/shard_map/all_gather | solution.py:205
  939.0 19.8 multiply_convert_fusion
  958.8 15.2 convolution_convert_fusion.1
  974.0 17.0 fusion.71
  991.0 16.1 multiply_reduce_fusion
  1019.8 165.6 %while.35 = (s32[]{:T(128)}, f32[2,2,480,128]{3,2,1,0:T(8,128)}, f32[1280,4,512]{2,1,0:T(4,128)}, s32[5]{0:T(128)S(1)}, s32[2,8]{1,0:T(2,128)S(1)}, /*index=5*/b...) while((s32[]{:T(128)}, f32[2,2,480,128]{3,2,1,0:T(8,128)}, ...), condition=%wide.region_12.13_spmd.clone, body=%wide.region_10.12_spmd.clone.sunk | while | flops 1270183168 | bytes 55970532 | solution.py:283
  1188.1 176.6 %all-reduce.15 = bf16[1280,4,512]{2,1,0:T(4,128)(2,1)} all-reduce(f32[1280,4,512]{2,1,0:T(4,128)} %get-tuple-element.344), channel_id=2, replica_groups=mesh['ctx'=4,'fsdp'=8] {'ctx','fsdp'}, use_global_device_ids=true, to_apply=%region_13.14.clone | all-reduce | flops 2621440 | bytes 15728640
  1380.7 23.8 %convolution_convert_fusion = bf16[1536,17920]{1,0:T(8,128)(2,1)} fusion(bf16[160,1536]{1,0:T(8,128)(2,1)S(1)} %copy-done.10, bf16[160,8960]{1,0:T(8,128)(2,1)} %get-tuple-element.485, bf16[160,8960]{1,0:T(8,128)(2,1)} %get-tuple-element.486), kind=kOutput, calls=%fused_computation.72 | convolution fusion | flops 8847032320 | bytes 61276160 | tf_op jit(solution)/shard_map/dot_general | solution.py:308
  1404.5 44.2 %pad_maximum_fusion = bf16[1536,21504]{1,0:T(8,128)(2,1)} fusion(bf16[1536,1536]{1,0:T(8,128)(2,1)} %convolution_convert_fusion.3, bf16[1536,2048]{1,0:T(8,128)(2,1)} %convolution_convert_fusion.2, bf16[1536,17920]{1,0:T(8,128)(2,1)} %convolution_convert_fusion), kind=kLoop, calls=%fused_computation.73 | loop fusion | flops 198180864 | bytes 132120576 | tf_op jit(solution)/shard_map/concatenate | solution.py:306
  1448.8 629.6 %reduce-scatter.3.cloned.1.call-done = bf16[192,21504]{1,0:T(8,128)(2,1)} async-done(((bf16[1536,21504]{1,0:T(8,128)(2,1)}), bf16[192,21504]{1,0:T(8,128)(2,1)}) %reduce-scatter.3.cloned.1.call-update) | async-done | bytes 8257552 | tf_op jit(solution)/shard_map/reduce_scatter | solution.py:305
  2080.4 16.4 fusion.44
  2107.0 26.1 %all-reduce.7 = (bf16[1536]{0:T(1024)(128)(2,1)S(1)}, bf16[1792]{0:T(1024)(128)(2,1)S(1)}, bf16[256]{0:T(256)(128)(2,1)S(1)}, bf16[1536]{0:T(1024)(128)(2,1)S(1)}) all-reduce(f32[1536]{0:T(1024)S(1)} %get-tuple-element.419, f32[1792]{0:T(1024)S(1)} %bitcast.253, ...), channel_id=3, replica_groups=mesh['ctx'=4,'fsdp'=8] {'fsdp'}, use_global_device_ids=true, to_apply=%region_16.17.clone | all-reduce | flops 5120 | bytes 30720
  2133.4 10.2 all-reduce.9
  2145.9 160.7 %all-reduce.14.cloned.1.call-done = (bf16[192,21504]{1,0:T(8,128)(2,1)}, bf16[1120,1536]{1,0:T(8,128)(2,1)}) async-done(((bf16[192,21504]{1,0:T(8,128)(2,1)}, bf16[1120,1536]{1,0:T(8,128)(2,1)}), (bf16[192,21504]{1,0:T(8,128)(2,1)}, bf16[1120,1536]{1,0:T(8,128)(2,1)})) %all-reduce.14.cloned.1.call-update) | async-done | bytes 11698192 | tf_op jit(solution)/shard_map/psum | solution.py:342
  (512 shorter events, 339.1 us)
Async XLA Ops:
  7.2 70.4 %all-gather.9.cloned.1.call-start = ((), (), s32[]{:S(2)}) async-start(), calls=%async_computation.2 | async-start | bytes 7077888 | tf_op jit(solution)/shard_map/all_gather | solution.py:122
  7.9 98.2 %all-gather.11.cloned.1.call-start = ((), (), s32[]{:S(2)}) async-start(), calls=%async_computation.3 | async-start | bytes 1474560 | tf_op jit(solution)/shard_map/all_gather | solution.py:150
  9.1 72.6 %copy-start = (f32[160,1536]{1,0:T(8,128)}, f32[160,1536]{1,0:T(8,128)S(1)}, u32[]{:S(2)}) copy-start(f32[160,1536]{1,0:T(8,128)S(1)} %reshape.608) | copy-start | bytes 2949124
  42.6 39.1 %copy-start.29 = (f32[1536]{0:T(1024)}, f32[1536]{0:T(1024)S(1)}, u32[]{:S(2)}) copy-start(f32[1536]{0:T(1024)S(1)} %convert_element_type.151) | copy-start | bytes 18436
  44.1 33.6 %copy-start.32 = (f32[160]{0:T(256)}, f32[160]{0:T(256)S(1)}, u32[]{:S(2)}) copy-start(f32[160]{0:T(256)S(1)} %rsqrt.20) | copy-start | bytes 1924
  45.6 36.7 %copy-start.26 = (f32[160,128]{1,0:T(8,128)}, f32[160,128]{1,0:T(8,128)S(1)}, u32[]{:S(2)}) copy-start(f32[160,128]{1,0:T(8,128)S(1)} %pad_maximum_fusion.4) | copy-start | bytes 245764
  46.4 35.7 %copy-start.24 = (f32[160,128]{1,0:T(8,128)}, f32[160,128]{1,0:T(8,128)S(1)}, u32[]{:S(2)}) copy-start(f32[160,128]{1,0:T(8,128)S(1)} %get-tuple-element.501) | copy-start | bytes 245764
  81.7 25.7 %copy-start.13 = (f32[160,2048]{1,0:T(8,128)}, f32[160,2048]{1,0:T(8,128)S(1)}, u32[]{:S(2)}) copy-start(f32[160,2048]{1,0:T(8,128)S(1)} %convolution_add_fusion.4) | copy-start | bytes 3932164
  83.9 84.9 %all-gather.13.cloned.1.call-start = ((), (), s32[]{:S(2)}) async-start(), calls=%async_computation.4 | async-start | bytes 6553600 | tf_op jit(solution)/shard_map/all_gather | solution.py:175
  106.1 147.5 %all-gather.15.cloned.1.call-start = ((), (), s32[]{:S(2)}) async-start(), calls=%async_computation.5 | async-start | bytes 5308416 | tf_op jit(solution)/shard_map/all_gather | solution.py:123
  106.7 354.3 %all-gather.17.cloned.1.call-start = ((), (), s32[]{:S(2)}) async-start(), calls=%async_computation.6 | async-start | bytes 30965760 | tf_op jit(solution)/shard_map/all_gather | solution.py:203
  107.3 592.6 %all-gather.19.cloned.1.call-start = ((), (), s32[]{:S(2)}) async-start(), calls=%async_computation.7 | async-start | bytes 30965760 | tf_op jit(solution)/shard_map/all_gather | solution.py:204
  107.9 831.1 %all-gather.21.cloned.1.call-start = ((), (), s32[]{:S(2)}) async-start(), calls=%async_computation.8 | async-start | bytes 30965760 | tf_op jit(solution)/shard_map/all_gather | solution.py:205
  108.7 1340.1 %reduce-scatter.5.cloned.1.call-start = ((), (), s32[]{:S(2)}) async-start(), calls=%async_computation.10 | async-start | bytes 30965760 | tf_op jit(solution)/shard_map/reduce_scatter | solution.py:327
  116.4 7.4 copy-start.15
  122.0 46.8 %copy-start.31 = (s32[2,8]{1,0:T(2,128)S(1)}, s32[2,8]{1,0:T(2,128)}, u32[]{:S(2)}) copy-start(s32[2,8]{1,0:T(2,128)} %param.16) | copy-start | bytes 196
  257.2 749.9 %copy-start.7 = (f32[160,1536]{1,0:T(8,128)}, f32[160,1536]{1,0:T(8,128)S(1)}, u32[]{:S(2)}) copy-start(f32[160,1536]{1,0:T(8,128)S(1)} %get-tuple-element.513) | copy-start | bytes 2949124
  257.4 442.5 %copy-start.9 = (bf16[160,1536]{1,0:T(8,128)(2,1)}, bf16[160,1536]{1,0:T(8,128)(2,1)S(1)}, u32[]{:S(2)}) copy-start(bf16[160,1536]{1,0:T(8,128)(2,1)S(1)} %multiply_convert_fusion.3) | copy-start | bytes 1474564
  477.3 461.7 %copy-start.16 = (bf16[160,1536]{1,0:T(8,128)(2,1)S(1)}, bf16[160,1536]{1,0:T(8,128)(2,1)}, u32[]{:S(2)}) copy-start(bf16[160,1536]{1,0:T(8,128)(2,1)} %reshape.600) | copy-start | bytes 1474564
  974.0 1104.4 %reduce-scatter.3.cloned.1.call-start = ((), (), s32[]{:S(2)}) async-start(), calls=%async_computation.9 | async-start | bytes 74317824 | tf_op jit(solution)/shard_map/reduce_scatter | solution.py:305
  1008.4 5.8 copy-start.17
  1369.8 5.8 copy-start.23
  1448.7 857.9 %all-reduce.14.cloned.1.call-start = ((), (), s32[]{:S(2)}) async-start(), calls=%async_computation.11 | async-start | bytes 23396352 | tf_op jit(solution)/shard_map/psum | solution.py:342
  2311.2 9.2 copy-start.19
  (29 other events, 90.2 us)
Sparse Core Ops, SparseCore 0:
  9.6 67.9 all-gather.8
  84.0 22.0 all-gather.10
  108.0 60.8 all-gather.12
  170.3 51.1 all-gather.14
  223.1 237.9 all-gather.16
  462.5 237.3 all-gather.18
  701.6 237.3 all-gather.20
  974.1 267.4 reduce-scatter.4
  1448.8 629.5 reduce-scatter.2
  2082.0 224.5 all-reduce.13
where the time goes:
time: 2340 us; the launch traced here: 2330 us
  waiting for transfers between devices  1540 us (66%)
  matrix products  274 us (12%)
  blocking collectives  242 us (10%)
  local copies, waits for them, and re-layouts  128 us (5%)
  other arithmetic  118 us (5%)
    reduce_scatter x1, waiting for transfers between devices, shards(): lax.psum_scatter(jnp.concatenate([lax.dot_general(normed_two, grad_gate_u...  630 us
    all_gather x1, waiting for transfers between devices, shards(): lax.all_gather(w_down, 'fsdp', axis=0, tiled=True)  223 us
    all_gather x1, waiting for transfers between devices, shards(): lax.all_gather(w_up, 'fsdp', axis=0, tiled=True)  223 us
    unnamed x3, blocking collectives  218 us
    all_gather x1, waiting for transfers between devices, shards(): lax.all_gather(w_gate, 'fsdp', axis=0, tiled=True)  204 us
    psum x1, waiting for transfers between devices, shards(): lax.psum(weight_rows.astype(jnp.bfloat16), 'ctx').astype(jnp.float32)  161 us
  transfers between devices with their start and end apart: 10, of which 8 were waited for; matrix products, arithmetic and copies ran while one was open for 20% of the time, Pallas kernels for 0%

commit v1 on v0

--- a/solution.py
+++ b/solution.py
@@ -18,6 +18,18 @@
 NEG_FILL = -1e30
 CONTRACT_LAST = (((1,), (1,)), ((), ()))
 CONTRACT_FIRST = (((0,), (0,)), ((), ()))
+
+
+def gather_by_bits(x, axis, dim):
+    ways, here = (lax.axis_size(axis), lax.axis_index(axis))
+    grown, reach = (x, 1)
+    while reach < ways:
+        theirs = lax.ppermute(grown, axis, [(d, d ^ reach) for d in range(ways)])
+        mine_first = jnp.concatenate([grown, theirs], axis=dim)
+        theirs_first = jnp.concatenate([theirs, grown], axis=dim)
+        grown = jnp.where(here & reach == 0, mine_first, theirs_first)
+        reach = 2 * reach
+    return grown
 
 
 def narrowed(values):
@@ -200,7 +212,7 @@
     unit_two, scale_two, normed = normalize(middle, gain_two)
     normed_two = normed.astype(jnp.bfloat16)
     gate_all, up_all, down_all = (
-        lax.all_gather(w_gate, "fsdp", axis=0, tiled=True),
+        gather_by_bits(w_gate, "fsdp", 0),
         lax.all_gather(w_up, "fsdp", axis=0, tiled=True),
         lax.all_gather(w_down, "fsdp", axis=0, tiled=True),
     )

time: 2340 us -> 2950 us (1.26)
  waiting for transfers between devices: 1540 us -> 2110 us
    ppermute x0 -> x3, waiting for transfers between devices: none -> 671 us  [gather_by_bits(): theirs = lax.ppermute(grown, axis, [(d, d ^ reach) for d in range(ways)])]
    all_gather x1, waiting for transfers between devices: 223 us -> 531 us  [shards(): lax.all_gather(w_up, 'fsdp', axis=0, tiled=True)]
    all_gather x1, waiting for transfers between devices: 204 us -> 0.02 us  [shards(): lax.all_gather(w_gate, 'fsdp', axis=0, tiled=True)]
    all_gather x1, waiting for transfers between devices: 223 us -> 64.7 us  [shards(): lax.all_gather(w_down, 'fsdp', axis=0, tiled=True)]
    all_gather x1, waiting for transfers between devices: 43.1 us -> 0.02 us  [shards(): lax.all_gather(block_kv, 'ctx', axis=0, tiled=True)]
  transfers between devices with their start and end apart: 10 -> 13, of which waited for: 8 -> 9; matrix products, arithmetic and copies ran while one was open for 20% -> 18% of each run, Pallas kernels for 0% -> 0%
where the time goes in v1:
time: 2950 us; the launch traced here: 2940 us
  waiting for transfers between devices  2110 us (72%)
  matrix products  279 us (9%)
  blocking collectives  241 us (8%)
  other arithmetic  143 us (5%)
  local copies, waits for them, and re-layouts  130 us (4%)
    ppermute x3, waiting for transfers between devices, gather_by_bits(): theirs = lax.ppermute(grown, axis, [(d, d ^ reach) for d in range(ways)])  671 us
    reduce_scatter x1, waiting for transfers between devices, shards(): lax.psum_scatter(jnp.concatenate([lax.dot_general(normed_two, grad_gate_u...  629 us
    all_gather x1, waiting for transfers between devices, shards(): lax.all_gather(w_up, 'fsdp', axis=0, tiled=True)  531 us
    unnamed x3, blocking collectives  218 us
    psum x1, waiting for transfers between devices, shards(): lax.psum(weight_rows.astype(jnp.bfloat16), 'ctx').astype(jnp.float32)  161 us
    all_gather x1, waiting for transfers between devices, shards(): lax.all_gather(w_down, 'fsdp', axis=0, tiled=True)  64.7 us
  transfers between devices with their start and end apart: 13, of which 9 were waited for; matrix products, arithmetic and copies ran while one was open for 18% of the time, Pallas kernels for 0%

profile of v1, /device:TPU:0, one launch (start us, length us, event | category | flops | bytes accessed | tf_op | source)
XLA Modules:
  0.0 2938.9 jit_solution(7707366536420569723)
XLA Ops:
  9.8 13.5 all-gather
  27.0 15.6 all-reduce.8
  46.4 31.2 %all-gather.9.cloned.1.call-done = bf16[1536,2048]{1,0:T(8,128)(2,1)} async-done(((bf16[192,2048]{1,0:T(8,128)(2,1)}), bf16[1536,2048]{1,0:T(8,128)(2,1)}) %all-gather.9.cloned.1.call-update) | async-done | bytes 6291472 | tf_op jit(solution)/shard_map/all_gather | solution.py:134
  84.0 22.2 all-gather.11.cloned.1.call-done
  127.9 304.0 %collective-permute-done.1 = bf16[384,8960]{1,0:T(8,128)(2,1)} collective-permute-done((bf16[384,8960]{1,0:T(8,128)(2,1)}, bf16[384,8960]{1,0:T(8,128)(2,1)}, u32[]{:S(2)}, u32[]{:S(2)}) %collective-permute-start.1) | collective-permute-done | bytes 6881312 | tf_op jit(solution)/shard_map/ppermute | solution.py:27
  431.8 16.4 maximum_select_fusion.2
  461.3 81.3 %while.34 = (s32[]{:T(128)}, f32[2,2,480]{2,1,0:T(2,128)S(1)}, f32[2,2,480]{2,1,0:T(2,128)S(1)}, f32[2,2,480,128]{3,2,1,0:T(8,128)}, s32[5]{0:T(128)S(1)}, /*ind...) while((s32[]{:T(128)}, f32[2,2,480]{2,1,0:T(2,128)S(1)}, ...), condition=%wide.region_6.7_spmd.clone, body=%wide.region_2.6_spmd.clone.sunk | while | flops 514415264 | bytes 27955316 | solution.py:206
  548.9 64.7 %all-gather.19.cloned.1.call-done = bf16[8960,1536]{1,0:T(8,128)(2,1)} async-done(((bf16[1120,1536]{1,0:T(8,128)(2,1)}), bf16[8960,1536]{1,0:T(8,128)(2,1)}) %all-gather.19.cloned.1.call-update) | async-done | bytes 27525136 | tf_op jit(solution)/shard_map/all_gather | solution.py:217
  613.6 17.1 fusion.78
  630.7 531.1 %all-gather.17.cloned.1.call-done = bf16[1536,8960]{1,0:T(8,128)(2,1)} async-done(((bf16[192,8960]{1,0:T(8,128)(2,1)}), bf16[1536,8960]{1,0:T(8,128)(2,1)}) %all-gather.17.cloned.1.call-update) | async-done | bytes 27525136 | tf_op jit(solution)/shard_map/all_gather | solution.py:216
  1161.8 15.6 fusion.77
  1177.3 360.9 %collective-permute-done.2 = bf16[768,8960]{1,0:T(8,128)(2,1)} collective-permute-done((bf16[768,8960]{1,0:T(8,128)(2,1)}, bf16[768,8960]{1,0:T(8,128)(2,1)}, u32[]{:S(2)}, u32[]{:S(2)}) %collective-permute-start.2) | collective-permute-done | bytes 13762592 | tf_op jit(solution)/shard_map/ppermute | solution.py:27
  1538.2 26.3 multiply_convert_fusion
  1564.5 14.7 convolution_convert_fusion.1
  1579.4 16.3 fusion.79
  1595.7 16.1 multiply_reduce_fusion
  1624.5 165.9 %while.35 = (s32[]{:T(128)}, f32[2,2,480,128]{3,2,1,0:T(8,128)}, f32[1280,4,512]{2,1,0:T(4,128)}, s32[5]{0:T(128)S(1)}, s32[2,8]{1,0:T(2,128)S(1)}, /*index=5*/b...) while((s32[]{:T(128)}, f32[2,2,480,128]{3,2,1,0:T(8,128)}, ...), condition=%wide.region_12.13_spmd.clone, body=%wide.region_10.12_spmd.clone.sunk | while | flops 1270183168 | bytes 54004424 | solution.py:295
  1793.1 176.1 %all-reduce.15 = bf16[1280,4,512]{2,1,0:T(4,128)(2,1)} all-reduce(f32[1280,4,512]{2,1,0:T(4,128)} %get-tuple-element.344), channel_id=2, replica_groups=mesh['ctx'=4,'fsdp'=8] {'ctx','fsdp'}, use_global_device_ids=true, to_apply=%region_13.14.clone | all-reduce | flops 2621440 | bytes 15728640
  1988.3 23.8 convolution_convert_fusion
  2012.1 44.2 %pad_maximum_fusion = bf16[1536,21504]{1,0:T(8,128)(2,1)} fusion(bf16[1536,1536]{1,0:T(8,128)(2,1)} %convolution_convert_fusion.3, bf16[1536,2048]{1,0:T(8,128)(2,1)} %convolution_convert_fusion.2, bf16[1536,17920]{1,0:T(8,128)(2,1)} %convolution_convert_fusion), kind=kLoop, calls=%fused_computation.73 | loop fusion | flops 198180864 | bytes 132120576 | tf_op jit(solution)/shard_map/concatenate | solution.py:318
  2056.4 629.3 %reduce-scatter.3.cloned.1.call-done = bf16[192,21504]{1,0:T(8,128)(2,1)} async-done(((bf16[1536,21504]{1,0:T(8,128)(2,1)}), bf16[192,21504]{1,0:T(8,128)(2,1)}) %reduce-scatter.3.cloned.1.call-update) | async-done | bytes 8257552 | tf_op jit(solution)/shard_map/reduce_scatter | solution.py:317
  2687.7 16.4 fusion.51
  2714.4 26.1 all-reduce.7
  2753.2 160.7 %all-reduce.14.cloned.1.call-done = (bf16[192,21504]{1,0:T(8,128)(2,1)}, bf16[1120,1536]{1,0:T(8,128)(2,1)}) async-done(((bf16[192,21504]{1,0:T(8,128)(2,1)}, bf16[1120,1536]{1,0:T(8,128)(2,1)}), (bf16[192,21504]{1,0:T(8,128)(2,1)}, bf16[1120,1536]{1,0:T(8,128)(2,1)})) %all-reduce.14.cloned.1.call-update) | async-done | bytes 11698192 | tf_op jit(solution)/shard_map/psum | solution.py:354
  (508 shorter events, 367.1 us)
Async XLA Ops:
  7.2 70.4 %all-gather.9.cloned.1.call-start = ((), (), s32[]{:S(2)}) async-start(), calls=%async_computation.2 | async-start | bytes 7077888 | tf_op jit(solution)/shard_map/all_gather | solution.py:134
  7.9 98.2 %all-gather.11.cloned.1.call-start = ((), (), s32[]{:S(2)}) async-start(), calls=%async_computation.3 | async-start | bytes 1474560 | tf_op jit(solution)/shard_map/all_gather | solution.py:162
  9.1 72.6 %copy-start = (f32[160,1536]{1,0:T(8,128)}, f32[160,1536]{1,0:T(8,128)S(1)}, u32[]{:S(2)}) copy-start(f32[160,1536]{1,0:T(8,128)S(1)} %reshape.608) | copy-start | bytes 2949124
  42.6 39.1 %copy-start.27 = (f32[1536]{0:T(1024)}, f32[1536]{0:T(1024)S(1)}, u32[]{:S(2)}) copy-start(f32[1536]{0:T(1024)S(1)} %convert_element_type.151) | copy-start | bytes 18436
  44.1 33.6 %copy-start.30 = (f32[160]{0:T(256)}, f32[160]{0:T(256)S(1)}, u32[]{:S(2)}) copy-start(f32[160]{0:T(256)S(1)} %rsqrt.20) | copy-start | bytes 1924
  45.6 36.7 %copy-start.25 = (f32[160,128]{1,0:T(8,128)}, f32[160,128]{1,0:T(8,128)S(1)}, u32[]{:S(2)}) copy-start(f32[160,128]{1,0:T(8,128)S(1)} %pad_maximum_fusion.4) | copy-start | bytes 245764
  46.4 35.7 %copy-start.24 = (f32[160,128]{1,0:T(8,128)}, f32[160,128]{1,0:T(8,128)S(1)}, u32[]{:S(2)}) copy-start(f32[160,128]{1,0:T(8,128)S(1)} %get-tuple-element.501) | copy-start | bytes 245764
  81.7 24.6 copy-start.11
  83.9 377.3 %all-gather.13.cloned.1.call-start = ((), (), s32[]{:S(2)}) async-start(), calls=%async_computation.4 | async-start | bytes 6553600 | tf_op jit(solution)/shard_map/all_gather | solution.py:187
  106.2 438.7 %all-gather.15.cloned.1.call-start = ((), (), s32[]{:S(2)}) async-start(), calls=%async_computation.5 | async-start | bytes 5308416 | tf_op jit(solution)/shard_map/all_gather | solution.py:135
  106.7 506.9 %all-gather.19.cloned.1.call-start = ((), (), s32[]{:S(2)}) async-start(), calls=%async_computation.7 | async-start | bytes 30965760 | tf_op jit(solution)/shard_map/all_gather | solution.py:217
  107.3 1054.5 %all-gather.17.cloned.1.call-start = ((), (), s32[]{:S(2)}) async-start(), calls=%async_computation.6 | async-start | bytes 30965760 | tf_op jit(solution)/shard_map/all_gather | solution.py:216
  107.9 1471.5 %all-gather.21.cloned.1.call-start = ((), (), s32[]{:S(2)}) async-start(), calls=%async_computation.8 | async-start | bytes 30965760 | tf_op jit(solution)/shard_map/all_gather | solution.py:226
  108.7 1947.8 %reduce-scatter.5.cloned.1.call-start = ((), (), s32[]{:S(2)}) async-start(), calls=%async_computation.10 | async-start | bytes 30965760 | tf_op jit(solution)/shard_map/reduce_scatter | solution.py:339
  108.7 6.3 collective-permute-start
  122.3 309.6 %collective-permute-start.1 = (bf16[384,8960]{1,0:T(8,128)(2,1)}, bf16[384,8960]{1,0:T(8,128)(2,1)}, u32[]{:S(2)}, u32[]{:S(2)}) collective-permute-start(bf16[384,8960]{1,0:T(8,128)(2,1)} %maximum_select_fusion.3), channel_id=1, source_target_pairs={{0,2},{1,3},{2,0},{3,1},{4,6},{5,7},{6,4},{7,5},{8,10},{9,11},{10,... | collective-permute-start | bytes 20643848 | tf_op jit(solution)/shard_map/ppermute | solution.py:27
  127.9 320.4 %copy-start.12 = (f32[160,2048]{1,0:T(8,128)S(1)}, f32[160,2048]{1,0:T(8,128)}, u32[]{:S(2)}) copy-start(f32[160,2048]{1,0:T(8,128)} %copy-done.11) | copy-start | bytes 3932164
  448.3 1089.9 %collective-permute-start.2 = (bf16[768,8960]{1,0:T(8,128)(2,1)}, bf16[768,8960]{1,0:T(8,128)(2,1)}, u32[]{:S(2)}, u32[]{:S(2)}) collective-permute-start(bf16[768,8960]{1,0:T(8,128)(2,1)} %maximum_select_fusion.2), channel_id=1, source_target_pairs={{0,4},{1,5},{2,6},{3,7},{4,0},{5,1},{6,2},{7,3},{8,12},{9,13},{10,... | collective-permute-start | bytes 41287688 | tf_op jit(solution)/shard_map/ppermute | solution.py:27
  544.3 69.4 %copy-start.6 = (bf16[160,1536]{1,0:T(8,128)(2,1)S(1)}, bf16[160,1536]{1,0:T(8,128)(2,1)}, u32[]{:S(2)}) copy-start(bf16[160,1536]{1,0:T(8,128)(2,1)} %reshape.600) | copy-start | bytes 1474564
  544.8 85.9 %copy-start.9 = (bf16[160,1536]{1,0:T(8,128)(2,1)}, bf16[160,1536]{1,0:T(8,128)(2,1)S(1)}, u32[]{:S(2)}) copy-start(bf16[160,1536]{1,0:T(8,128)(2,1)S(1)} %convert_element_type.162) | copy-start | bytes 1474564
  548.7 1063.1 %copy-start.7 = (f32[160,1536]{1,0:T(8,128)}, f32[160,1536]{1,0:T(8,128)S(1)}, u32[]{:S(2)}) copy-start(f32[160,1536]{1,0:T(8,128)S(1)} %get-tuple-element.513) | copy-start | bytes 2949124
  548.9 989.3 %copy-start.14 = (bf16[160,1536]{1,0:T(8,128)(2,1)}, bf16[160,1536]{1,0:T(8,128)(2,1)S(1)}, u32[]{:S(2)}) copy-start(bf16[160,1536]{1,0:T(8,128)(2,1)S(1)} %multiply_convert_fusion.3) | copy-start | bytes 1474564
  1579.3 1106.4 %reduce-scatter.3.cloned.1.call-start = ((), (), s32[]{:S(2)}) async-start(), calls=%async_computation.9 | async-start | bytes 74317824 | tf_op jit(solution)/shard_map/reduce_scatter | solution.py:317
  2056.3 857.5 %all-reduce.14.cloned.1.call-start = ((), (), s32[]{:S(2)}) async-start(), calls=%async_computation.11 | async-start | bytes 23396352 | tf_op jit(solution)/shard_map/psum | solution.py:354
  (26 other events, 93.9 us)
Sparse Core Ops, SparseCore 0:
  9.6 67.9 all-gather.8
  84.0 22.0 all-gather.10
  108.0 60.8 all-gather.12
  170.3 84.2 all-gather.14
  256.1 357.4 all-gather.18
  615.1 546.6 all-gather.16
  1163.4 349.4 all-gather.20
  1579.4 268.8 reduce-scatter.4
  2056.5 629.1 reduce-scatter.2
  2689.3 224.4 all-reduce.13
